TPU v7x, 16 devices: a whole 2x2x2 slice. The times are simulated.
16 devices in a mesh: dp: 4 (over z, y), tp: 4 (over x, core).
Axes of the slice: x: 2, y: 2, z: 2, core: 2. Of those that a mesh axis runs over, the one named last changes fastest.
Arguments:
- hidden: bfloat16 [8, 1024, 5120], P('dp', 'tp'), parts along dimension 0
- positions: int32 [8, 1024], P('dp'), parts along dimension 0
- gain_attn: bfloat16 [5120], replicated
- w_q: bfloat16 [5120, 5120], P(None, 'tp')
- b_q: bfloat16 [5120], P('tp')
- w_k: bfloat16 [5120, 1024], P(None, 'tp')
- b_k: bfloat16 [1024], P('tp')
- w_v: bfloat16 [5120, 1024], P(None, 'tp')
- b_v: bfloat16 [1024], P('tp')
- w_o: bfloat16 [5120, 5120], P('tp')
- gain_mlp: bfloat16 [5120], replicated
- w_gate: bfloat16 [5120, 27648], P(None, 'tp')
- w_up: bfloat16 [5120, 27648], P(None, 'tp')
- w_down: bfloat16 [27648, 5120], P('tp')
Outputs:
- output 1: bfloat16 [8, 1024, 5120], P('dp', 'tp'), parts along dimension 0
- output 2: bfloat16 [8, 1024, 8, 128], P('dp', None, 'tp'), parts along dimension 0
- output 3: bfloat16 [8, 1024, 8, 128], P('dp', None, 'tp'), parts along dimension 0
There are 4 independent parts. A program takes and returns all parts, laid end to end along the dimension named above; an argument that names none is the same for every part.
All inputs are finite; a program needn't handle non-finite values.
Results may differ from a plain program's by a relative error of at most 0.0130781.
Values are sent between devices in bfloat16 or wider.
A program may use at most 1 GiB of HBM per device.

v0:
```python
import jax
import jax.numpy as jnp
from jax import lax
from jax.sharding import PartitionSpec as P, NamedSharding

HEAD_DIM = 128
ROPE_THETA = 1000000.0
NORM_EPS = 1e-6


def rms_norm(values, gain):
    values_f32 = values.astype(jnp.float32)
    inv_rms = lax.rsqrt(jnp.mean(values_f32 * values_f32, axis=-1, keepdims=True) + NORM_EPS)
    return (values_f32 * inv_rms * gain.astype(jnp.float32)).astype(jnp.bfloat16)


def rotary(values, positions):
    half_dim = HEAD_DIM // 2
    inv_freq = ROPE_THETA ** (-jnp.arange(half_dim, dtype=jnp.float32) / half_dim)
    angles = positions.astype(jnp.float32)[:, :, None] * inv_freq
    angles = angles.reshape(angles.shape[:2] + (1,) * (values.ndim - 3) + (half_dim,))
    cosine = jnp.cos(angles)
    sine = jnp.sin(angles)
    first = values[..., :half_dim]
    second = values[..., half_dim:]
    return jnp.concatenate([first * cosine - second * sine, second * cosine + first * sine], axis=-1)


def project(normed, weight, bias):
    return jnp.einsum('btd,df->btf', normed, weight, preferred_element_type=jnp.float32) + bias.astype(jnp.float32)


def attention(query, key_heads, value_heads):
    seq_len = query.shape[1]
    causal = jnp.arange(seq_len)[:, None] >= jnp.arange(seq_len)[None, :]
    scores = jnp.einsum('btkgd,bskd->bkgts', query, key_heads, preferred_element_type=jnp.float32) * (HEAD_DIM ** -0.5)
    scores = jnp.where(causal, scores, -1e30)
    attn_probs = jax.nn.softmax(scores, axis=-1).astype(jnp.bfloat16)
    attn_out = jnp.einsum('bkgts,bskd->btkgd', attn_probs, value_heads, preferred_element_type=jnp.float32)
    return attn_out.astype(jnp.bfloat16).reshape(query.shape[0], seq_len, -1)


def solution(mesh):
    def local_layer(hidden, positions, gain_attn, w_q, b_q, w_k, b_k, w_v, b_v, w_o, gain_mlp, w_gate, w_up, w_down):
        batch = hidden.shape[0]
        seq_len = positions.shape[1]
        kv_local = w_k.shape[1] // HEAD_DIM
        group = w_q.shape[1] // w_k.shape[1]
        normed = rms_norm(hidden, gain_attn)
        normed_all = lax.all_gather(normed, 'tp', axis=1, tiled=True)
        query = project(normed_all, w_q, b_q).reshape(batch, seq_len, kv_local, group, HEAD_DIM)
        query = rotary(query, positions).astype(jnp.bfloat16)
        key_proj = project(normed_all, w_k, b_k).reshape(batch, seq_len, kv_local, HEAD_DIM)
        k_cache = rotary(key_proj, positions).astype(jnp.bfloat16)
        v_cache = project(normed_all, w_v, b_v).reshape(batch, seq_len, kv_local, HEAD_DIM).astype(jnp.bfloat16)
        attn_out = attention(query, k_cache, v_cache)
        attn_part = jnp.einsum('btf,fd->btd', attn_out, w_o, preferred_element_type=jnp.float32).astype(jnp.bfloat16)
        attn_sum = lax.psum_scatter(attn_part, 'tp', scatter_dimension=1, tiled=True)
        hidden_mid = (hidden.astype(jnp.float32) + attn_sum.astype(jnp.float32)).astype(jnp.bfloat16)
        normed_mid = rms_norm(hidden_mid, gain_mlp)
        normed_mid_all = lax.all_gather(normed_mid, 'tp', axis=1, tiled=True)
        gate = jnp.einsum('btd,df->btf', normed_mid_all, w_gate, preferred_element_type=jnp.float32)
        up_proj = jnp.einsum('btd,df->btf', normed_mid_all, w_up, preferred_element_type=jnp.float32)
        activation = (jax.nn.silu(gate) * up_proj).astype(jnp.bfloat16)
        down_part = jnp.einsum('btf,fd->btd', activation, w_down, preferred_element_type=jnp.float32).astype(jnp.bfloat16)
        down_sum = lax.psum_scatter(down_part, 'tp', scatter_dimension=1, tiled=True)
        hidden_out = (hidden_mid.astype(jnp.float32) + down_sum.astype(jnp.float32)).astype(jnp.bfloat16)
        return hidden_out, k_cache, v_cache

    token_rows = P('dp', 'tp', None)
    col_split = P(None, 'tp')
    row_split = P('tp', None)
    vec_split = P('tp')
    replicated = P(None)
    cache_spec = P('dp', None, 'tp', None)
    in_specs = (token_rows, P('dp', None), replicated, col_split, vec_split, col_split, vec_split, col_split, vec_split, row_split, replicated, col_split, col_split, row_split)
    out_specs = (token_rows, cache_spec, cache_spec)
    return jax.shard_map(local_layer, mesh=mesh, in_specs=in_specs, out_specs=out_specs, check_vma=False)
```

profile of v0, /device:TPU:0, one launch (start us, length us, event | category | flops | bytes accessed | tf_op | source)
XLA Modules:
  0.0 1326.6 jit_solution(7492395083014109749)
XLA Ops:
  7.3 3.7 fusion.19
  11.7 6.8 fusion.21
  19.2 1.3 iota_compare_fusion
  20.5 6.0 multiply_cosine_fusion
  26.6 123.3 %all-gather.3.cloned.1.call-done = bf16[2,1024,5120]{2,1,0:T(8,128)(2,1)} async-done(((bf16[2,256,5120]{2,1,0:T(8,128)(2,1)}), bf16[2,1024,5120]{2,1,0:T(8,128)(2,1)}) %all-gather.3.cloned.1.call-update) | async-done | bytes 20971536 | tf_op jit(solution)/shard_map/all_gather | solution.py:50
  149.9 35.5 %fusion.29 = f32[2,1024,1280]{2,1,0:T(8,128)} fusion(bf16[2,1024,5120]{2,1,0:T(8,128)(2,1)} %all-gather.3.cloned.1.call-done, bf16[5120,1280]{1,0:T(8,128)(2,1)} %param.17, f32[1280]{0:T(1024)S(1)} %convert_element_type.79), kind=kOutput, calls=%fused_computation.39 | convolution fusion | flops 26846167040 | bytes 44569600 | tf_op jit(solution)/shard_map/btd,df->btf/dot_general | solution.py:30
  185.4 11.3 copy.31
  196.7 9.9 fusion.39
  206.9 10.3 fusion.56
  217.2 1.9 copy.47
  219.1 2.1 copy.46
  221.2 8.4 copy.49
  229.6 8.7 copy.48
  238.4 2.9 subtract_convert_fusion.1
  241.3 1.5 pad_maximum_fusion.1
  244.0 10.2 subtract_convert_fusion
  254.1 38.4 %fusion.58 = (f32[2,2,5,1024]{3,2,1,0:T(8,128)S(1)}, f32[2,2,5,1024,1024]{3,4,2,1,0:T(8,128)}) fusion(pred[1024,1024]{0,1:T(8,128)(4,1)} %iota_compare_fusion, bf16[2,1024,2,128]{3,1,2,0:T(8,128)(2,1)} %pad_maximum_fusion.1, bf16[2,1024,2,5,64]{4,1,3,2,0:T(8,128)(2,1)} %get-tuple-element.10, bf16[2,1024,2,5,64]{4,1,3,2,0:T(8,128)(2,1)} %get-tuple-element.9), kind=kOutput, calls=%fused_computation.67 | convolution fusion | flops 5463081984 | bytes 91308032 | tf_op jit(solution)/shard_map/sub | solution.py:38
  292.5 10.7 add_convert_fusion.2
  303.2 29.6 %fusion.32 = bf16[2,2,128,5,1024]{4,2,3,1,0:T(8,128)(2,1)} fusion(bf16[2,1024,2,128,1]{1,3,4,2,0:T(8,128)(2,1)S(1)} %bitcast.75, f32[2,2,5,1024,1024]{3,4,2,1,0:T(8,128)} %get-tuple-element.20, f32[2,2,5,1024]{3,2,1,0:T(8,128)S(1)} %get-tuple-element.19), kind=kOutput, calls=%fused_computation.42 | convolution fusion | flops 5413273600 | bytes 90259456 | tf_op jit(solution)/shard_map/bkgts,bskd->btkgd/dot_general | solution.py:39
  332.8 34.5 %convolution_convert_fusion = bf16[2,1024,5120]{2,1,0:T(8,128)(2,1)} fusion(bf16[2,1024,1280]{1,2,0:T(8,128)(2,1)} %bitcast.77, bf16[1280,5120]{1,0:T(8,128)(2,1)} %param.23), kind=kOutput, calls=%fused_computation.23 | convolution fusion | flops 26854031360 | bytes 39321600 | tf_op jit(solution)/shard_map/btf,fd->btd/dot_general | solution.py:57
  368.0 145.2 %reduce-scatter.3.cloned.1.call-done = bf16[2,256,5120]{2,1,0:T(8,128)(2,1)} async-done(((bf16[2,1024,5120]{2,1,0:T(8,128)(2,1)}), bf16[2,256,5120]{2,1,0:T(8,128)(2,1)}) %reduce-scatter.3.cloned.1.call-update) | async-done | bytes 5242896 | tf_op jit(solution)/shard_map/reduce_scatter | solution.py:58
  513.3 6.0 fusion.23
  519.2 7.5 fusion.25
  526.8 128.5 %all-gather.5.cloned.1.call-done = bf16[2,1024,5120]{2,1,0:T(8,128)(2,1)} async-done(((bf16[2,256,5120]{2,1,0:T(8,128)(2,1)}), bf16[2,1024,5120]{2,1,0:T(8,128)(2,1)}) %all-gather.5.cloned.1.call-update) | async-done | bytes 20971536 | tf_op jit(solution)/shard_map/all_gather | solution.py:61
  655.3 170.2 %fusion.3 = f32[2,1024,6912]{2,1,0:T(8,128)} fusion(bf16[2,1024,5120]{2,1,0:T(8,128)(2,1)} %all-gather.5.cloned.1.call-done, bf16[5120,6912]{1,0:T(8,128)(2,1)} %param.26), kind=kOutput, calls=%fused_computation.6 | convolution fusion | flops 144955146240 | bytes 148373504 | tf_op jit(solution)/shard_map/btd,df->btf/dot_general | solution.py:63
  825.5 169.7 %fusion.5 = f32[2,1024,6912]{2,1,0:T(8,128)} fusion(bf16[2,1024,5120]{2,1,0:T(8,128)(2,1)} %all-gather.5.cloned.1.call-done, bf16[5120,6912]{1,0:T(8,128)(2,1)} %param.25), kind=kOutput, calls=%fused_computation.8 | convolution fusion | flops 144955146240 | bytes 148373504 | tf_op jit(solution)/shard_map/btd,df->btf/dot_general | solution.py:62
  995.2 167.8 %fusion.13 = bf16[2,1024,5120]{2,1,0:T(8,128)(2,1)} fusion(bf16[6912,5120]{1,0:T(8,128)(2,1)} %param.27, f32[2,1024,6912]{2,1,0:T(8,128)} %fusion.3, f32[2,1024,6912]{2,1,0:T(8,128)} %fusion.5), kind=kOutput, calls=%fused_computation.24 | convolution fusion | flops 145050566656 | bytes 204996608 | tf_op jit(solution)/shard_map/btf,fd->btd/dot_general | solution.py:65
  1163.0 1.2 copy-done.6
  1164.2 2.0 copy.36
  1166.2 3.8 copy.37
  1170.0 138.9 %reduce-scatter.5.cloned.1.call-done = bf16[2,256,5120]{2,1,0:T(8,128)(2,1)} async-done(((bf16[2,1024,5120]{2,1,0:T(8,128)(2,1)}), bf16[2,256,5120]{2,1,0:T(8,128)(2,1)}) %reduce-scatter.5.cloned.1.call-update) | async-done | bytes 5242896 | tf_op jit(solution)/shard_map/reduce_scatter | solution.py:66
  1308.9 10.9 fusion.26
  (45 shorter events, 3.6 us)
Async XLA Ops:
  7.2 189.5 %copy-start = (bf16[5120,256]{1,0:T(8,128)(2,1)S(1)}, bf16[5120,256]{1,0:T(8,128)(2,1)}, u32[]{:S(2)}) copy-start(bf16[5120,256]{1,0:T(8,128)(2,1)} %param.19) | copy-start | bytes 7864324
  7.2 11.4 copy-start.11
  7.2 11.4 copy-start.12
  7.2 12.0 copy-start.9
  7.2 12.0 copy-start.10
  7.2 142.7 %all-gather.3.cloned.1.call-start = ((), (), s32[]{:S(2)}) async-start(), calls=%async_computation.2 | async-start | bytes 26214400 | tf_op jit(solution)/shard_map/all_gather | solution.py:50
  18.5 494.7 %reduce-scatter.3.cloned.1.call-start = ((), (), s32[]{:S(2)}) async-start(), calls=%async_computation.3 | async-start | bytes 26214400 | tf_op jit(solution)/shard_map/reduce_scatter | solution.py:58
  229.6 8.8 copy-start.4
  229.6 8.8 copy-start.5
  238.3 5.6 copy-start.3
  254.1 38.4 %copy-start.13 = (f32[256]{0:T(256)S(1)}, f32[256]{0:T(256)}, u32[]{:S(2)}) copy-start(f32[256]{0:T(256)} %convert_element_type.74) | copy-start | bytes 3076
  303.2 29.6 %copy-start.7 = (bf16[2,1024,256]{1,2,0:T(8,128)(2,1)}, bf16[2,1024,256]{1,2,0:T(8,128)(2,1)S(1)}, u32[]{:S(2)}) copy-start(bf16[2,1024,256]{1,2,0:T(8,128)(2,1)S(1)} %add_convert_fusion.2) | copy-start | bytes 3145732
  367.3 0.7 copy-start.8
  367.4 287.9 %all-gather.5.cloned.1.call-start = ((), (), s32[]{:S(2)}) async-start(), calls=%async_computation.4 | async-start | bytes 26214400 | tf_op jit(solution)/shard_map/all_gather | solution.py:61
  513.3 6.0 copy-start.2
  526.7 782.2 %reduce-scatter.5.cloned.1.call-start = ((), (), s32[]{:S(2)}) async-start(), calls=%async_computation.5 | async-start | bytes 26214400 | tf_op jit(solution)/shard_map/reduce_scatter | solution.py:66
  1162.9 1.2 copy-start.6
  1166.2 153.7 %copy-start.1 = (bf16[5120,256]{1,0:T(8,128)(2,1)S(1)}, bf16[5120,256]{1,0:T(8,128)(2,1)}, u32[]{:S(2)}) copy-start(bf16[5120,256]{1,0:T(8,128)(2,1)} %param.19) | copy-start | bytes 7864324
Sparse Core Ops, SparseCore 0:
  18.7 131.1 all-gather.2
  367.5 145.7 reduce-scatter.2
  526.9 128.3 all-gather.4
  1163.1 145.7 reduce-scatter.4
where the time goes:
time: 1330 us
  matrix products  666 us (50%)
  waiting for transfers between devices  536 us (40%)
  other arithmetic  58.2 us (4%)
  local copies, waits for them, and re-layouts  51.8 us (4%)
  between operations  14.1 us (1%)
    dot_general x1, matrix products, local_layer(): jnp.einsum('btd,df->btf', normed_mid_all, w_up, preferred_element_type=jn...  170 us
    dot_general x1, matrix products, local_layer(): jnp.einsum('btd,df->btf', normed_mid_all, w_gate, preferred_element_type=...  170 us
    dot_general x1, matrix products, local_layer(): jnp.einsum('btf,fd->btd', activation, w_down, preferred_element_type=jnp....  168 us
    reduce_scatter x1, waiting for transfers between devices, local_layer(): lax.psum_scatter(attn_part, 'tp', scatter_dimension=1, tiled=True)  145 us
    reduce_scatter x1, waiting for transfers between devices, local_layer(): lax.psum_scatter(down_part, 'tp', scatter_dimension=1, tiled=True)  139 us
    all_gather x1, waiting for transfers between devices, local_layer(): normed_mid_all = lax.all_gather(normed_mid, 'tp', axis=1, tiled=True)  128 us
    all_gather x1, waiting for transfers between devices, local_layer(): normed_all = lax.all_gather(normed, 'tp', axis=1, tiled=True)  123 us
    dot_general x3, matrix products, project(): jnp.einsum('btd,df->btf', normed, weight, preferred_element_type=jnp.floa...  56.1 us
  transfers between devices with their start and end apart: 4, of which 4 were waited for; matrix products, arithmetic and copies ran while one was open for 1% of the time, Pallas kernels for 0%

commit v1 on v0

v1 whole, which is shorter than its diff:
```python
import functools

import jax
import jax.numpy as jnp
from jax import lax
from jax.experimental import pallas as pl
from jax.experimental.pallas import tpu as pltpu
from jax.sharding import PartitionSpec as P

HEAD_DIM = 128
ROPE_THETA = 1000000.0
NORM_EPS = 1e-6
Q_BLOCK = 256
DOWN_SPLIT = 4


def rms_norm(values, gain):
    values_f32 = values.astype(jnp.float32)
    inv_rms = lax.rsqrt(jnp.mean(values_f32 * values_f32, axis=-1, keepdims=True) + NORM_EPS)
    return (values_f32 * inv_rms * gain.astype(jnp.float32)).astype(jnp.bfloat16)


def rope_tables(positions):
    half_dim = HEAD_DIM // 2
    inv_freq = ROPE_THETA ** (-jnp.arange(half_dim, dtype=jnp.float32) / half_dim)
    angles = positions.astype(jnp.float32)[:, None] * inv_freq
    cosine = jnp.cos(angles)
    sine = jnp.sin(angles)
    return jnp.concatenate([cosine, cosine], axis=-1), jnp.concatenate([-sine, sine], axis=-1)


def attention_kernel(cos_ref, sin_ref, q_ref, k_ref, v_ref, o_ref, k_out_ref, q_rot):
    seq_len = q_ref.shape[0]

    def rotate(values):
        return values * cos_ref[...] + pltpu.roll(values, HEAD_DIM // 2, 1) * sin_ref[...]

    @pl.when(pl.program_id(1) == 0)
    def _():
        k_out_ref[...] = rotate(k_ref[...]).astype(jnp.bfloat16)

    q_rot[...] = rotate(q_ref[...]).astype(jnp.bfloat16)
    scale = HEAD_DIM ** -0.5
    dims = (((1,), (1,)), ((), ()))
    rows = lax.broadcasted_iota(jnp.int32, (Q_BLOCK, Q_BLOCK), 0)
    cols = lax.broadcasted_iota(jnp.int32, (Q_BLOCK, Q_BLOCK), 1)
    causal = rows >= cols
    for i in range(seq_len // Q_BLOCK):
        lo, hi = i * Q_BLOCK, (i + 1) * Q_BLOCK
        q = q_rot[lo:hi, :]
        diag = lax.dot_general(q, k_out_ref[lo:hi, :], dims, preferred_element_type=jnp.float32) * scale
        diag = jnp.where(causal, diag, -1e30)
        top = jnp.max(diag, axis=-1, keepdims=True)
        if i:
            past = lax.dot_general(q, k_out_ref[:lo, :], dims, preferred_element_type=jnp.float32) * scale
            top = jnp.maximum(top, jnp.max(past, axis=-1, keepdims=True))
        diag = jnp.exp(diag - top)
        norm = jnp.sum(diag, axis=-1, keepdims=True)
        if i:
            past = jnp.exp(past - top)
            norm = norm + jnp.sum(past, axis=-1, keepdims=True)
        inv = 1.0 / norm
        out = jnp.dot((diag * inv).astype(jnp.bfloat16), v_ref[lo:hi, :], preferred_element_type=jnp.float32)
        if i:
            out = out + jnp.dot((past * inv).astype(jnp.bfloat16), v_ref[:lo, :], preferred_element_type=jnp.float32)
        o_ref[lo:hi, :] = out.astype(jnp.bfloat16)


def attention(cosine, sine, query, key, value):
    seq_len, q_width = query.shape
    kv_width = key.shape[1]
    group = q_width // kv_width
    kv_heads = kv_width // HEAD_DIM
    full = pl.BlockSpec((seq_len, HEAD_DIM), lambda h, g: (0, 0))
    per_q = pl.BlockSpec((seq_len, HEAD_DIM), lambda h, g: (0, h * group + g))
    per_kv = pl.BlockSpec((seq_len, HEAD_DIM), lambda h, g: (0, h))
    return pl.pallas_call(
        attention_kernel,
        grid=(kv_heads, group),
        in_specs=[full, full, per_q, per_kv, per_kv],
        out_specs=[per_q, per_kv],
        out_shape=[jax.ShapeDtypeStruct((seq_len, q_width), jnp.bfloat16),
                   jax.ShapeDtypeStruct((seq_len, kv_width), jnp.bfloat16)],
        scratch_shapes=[pltpu.VMEM((seq_len, HEAD_DIM), jnp.bfloat16)],
        compiler_params=pltpu.CompilerParams(vmem_limit_bytes=32 * 1024 * 1024),
        cost_estimate=pl.CostEstimate(flops=16 * seq_len * seq_len * q_width, bytes_accessed=8 * seq_len * q_width, transcendentals=0),
        name="attention",
    )(cosine, sine, query, key, value)


def after(value, *others):
    return lax.optimization_barrier((value,) + others)[0]


def dot(left, right):
    return jnp.dot(left, right, preferred_element_type=jnp.float32)


def solution(mesh):
    def local_layer(hidden, positions, gain_attn, w_q, b_q, w_k, b_k, w_v, b_v, w_o, gain_mlp, w_gate, w_up, w_down):
        batch = hidden.shape[0]
        seq_len = positions.shape[1]
        kv_local = w_k.shape[1] // HEAD_DIM
        width = hidden.shape[2]

        def gather(part):
            return lax.all_gather(part, 'tp', axis=0, tiled=True)

        def scatter(part):
            return lax.psum_scatter(part, 'tp', scatter_dimension=0, tiled=True)

        def bias(vec):
            return vec.astype(jnp.float32)

        def add(res, total):
            return (res.astype(jnp.float32) + total.astype(jnp.float32)).astype(jnp.bfloat16)

        def qkv_attention(x, tables):
            query = dot(x, w_q) + bias(b_q)
            key = dot(x, w_k) + bias(b_k)
            value = (dot(x, w_v) + bias(b_v)).astype(jnp.bfloat16)
            out, key = attention(tables[0], tables[1], query, key, value)
            return out, key, value

        tables = [rope_tables(positions[b]) for b in range(batch)]
        normed0 = rms_norm(hidden[0], gain_attn)
        x0 = gather(normed0)
        normed1 = rms_norm(after(hidden[1], normed0), gain_attn)
        x1 = gather(normed1)
        o0, k0, v0 = qkv_attention(x0, tables[0])
        rows = hidden.shape[1]
        half = rows // 2

        def half_of(values, i):
            parts = values.reshape(seq_len // rows, rows, -1)
            return parts[:, i * half:(i + 1) * half].reshape(seq_len // 2, -1)

        part00 = dot(half_of(o0, 0), w_o).astype(jnp.bfloat16)
        sum00 = scatter(part00)
        part01 = dot(after(half_of(o0, 1), part00), w_o).astype(jnp.bfloat16)
        sum01 = scatter(part01)
        o1, k1, v1 = qkv_attention(after(x1, part01), tables[1])
        mid00 = add(hidden[0, :half], after(sum00, o1))
        h00 = rms_norm(mid00, gain_mlp)
        y00 = gather(h00)
        mid01 = add(hidden[0, half:], after(sum01, h00))
        h01 = rms_norm(mid01, gain_mlp)
        y01 = gather(h01)
        part1 = dot(after(o1, h01), w_o).astype(jnp.bfloat16)
        sum1 = scatter(part1)
        y00 = after(y00, part1)
        gate00 = dot(y00, w_gate)
        up00 = dot(after(y00, gate00), w_up)
        act00 = (jax.nn.silu(gate00) * up00).astype(jnp.bfloat16)
        y01 = after(y01, act00)
        gate01 = dot(y01, w_gate)
        mid1 = add(hidden[1], after(sum1, gate01))
        h1 = rms_norm(mid1, gain_mlp)
        y1 = gather(h1)
        up01 = dot(after(y01, h1), w_up)
        act01 = (jax.nn.silu(gate01) * up01).astype(jnp.bfloat16)
        down00 = dot(after(act00, act01), w_down).astype(jnp.bfloat16)
        total00 = scatter(after(down00, y1))
        down0 = dot(after(act01, down00), w_down).astype(jnp.bfloat16)
        total0 = scatter(after(down0, total00))
        y1 = after(y1, down0)
        gate1 = dot(y1, w_gate)
        up1 = dot(y1, w_up)
        act1 = (jax.nn.silu(gate1) * up1).astype(jnp.bfloat16)
        out0 = jnp.concatenate([add(mid00, after(total00, act1)), add(mid01, after(total0, act1))], axis=0)
        step = width // DOWN_SPLIT
        outs = []
        previous = total0
        for i in range(DOWN_SPLIT):
            cols = slice(i * step, (i + 1) * step)
            down = dot(act1, w_down[:, cols]).astype(jnp.bfloat16)
            act1 = after(act1, down)
            previous = scatter(after(down, previous))
            outs.append(add(mid1[:, cols], previous))
        out1 = jnp.concatenate(outs, axis=1)
        shape = (seq_len, kv_local, HEAD_DIM)
        stack = lambda a, b: jnp.stack([a.reshape(shape), b.reshape(shape)])
        return jnp.stack([out0, out1]), stack(k0, k1), stack(v0, v1)

    token_rows = P('dp', 'tp', None)
    col_split = P(None, 'tp')
    row_split = P('tp', None)
    vec_split = P('tp')
    replicated = P(None)
    cache_spec = P('dp', None, 'tp', None)
    in_specs = (token_rows, P('dp', None), replicated, col_split, vec_split, col_split, vec_split, col_split, vec_split, row_split, replicated, col_split, col_split, row_split)
    out_specs = (token_rows, cache_spec, cache_spec)
    return jax.shard_map(local_layer, mesh=mesh, in_specs=in_specs, out_specs=out_specs, check_vma=False)
```

time: 1330 us -> 926 us (0.70)
  waiting for transfers between devices: 536 us -> 138 us
  Pallas kernels: 0 us -> 49.5 us
  local copies, waits for them, and re-layouts: 51.8 us -> 7.53 us
    reduce_scatter x2 -> x9, waiting for transfers between devices: 284 us -> 63.3 us  [scatter(): return lax.psum_scatter(part, 'tp', scatter_dimension=0, tiled=True)]
    all_gather x2 -> x5, waiting for transfers between devices: 252 us -> 74.9 us  [gather(): return lax.all_gather(part, 'tp', axis=0, tiled=True)]
    pallas_call x0 -> x2, Pallas kernels: none -> 49.5 us  [attention(): pl.pallas_call(attention_kernel, grid=(kv_heads, group), in_specs=[full,...]
    sub x1 -> x0, matrix products: 38.4 us -> none  [attention(): attn_probs = jax.nn.softmax(scores, axis=-1).astype(jnp.bfloat16)]
    dot_general x8 -> x21, matrix products: 628 us -> 659 us  [dot(): return jnp.dot(left, right, preferred_element_type=jnp.float32)]
    unnamed x34 -> x72, local copies, waits for them, and re-layouts: 30 us -> 3.86 us
  transfers between devices with their start and end apart: 4 -> 14, of which waited for: 4 -> 7; matrix products, arithmetic and copies ran while one was open for 1% -> 75% of each run, Pallas kernels for 0% -> 5%
where the time goes in v1:
time: 926 us; the launch traced here: 923 us
  matrix products  659 us (71%)
  waiting for transfers between devices  138 us (15%)
  other arithmetic  52.5 us (6%)
  Pallas kernels  49.5 us (5%)
  between operations  14.7 us (2%)
    dot_general x21, matrix products, dot(): return jnp.dot(left, right, preferred_element_type=jnp.float32)  659 us
    all_gather x5, waiting for transfers between devices, gather(): return lax.all_gather(part, 'tp', axis=0, tiled=True)  74.9 us
    reduce_scatter x9, waiting for transfers between devices, scatter(): return lax.psum_scatter(part, 'tp', scatter_dimension=0, tiled=True)  63.3 us
    pallas_call x2, Pallas kernels, attention(): pl.pallas_call(attention_kernel, grid=(kv_heads, group), in_specs=[full,...  49.5 us
  transfers between devices with their start and end apart: 14, of which 7 were waited for; matrix products, arithmetic and copies ran while one was open for 75% of the time, Pallas kernels for 5%

profile of v1, /device:TPU:0, one launch (start us, length us, event | category | flops | bytes accessed | tf_op | source)
XLA Modules:
  0.0 922.7 jit_solution(11417939356163944448)
XLA Ops:
  19.9 5.0 fusion.41
  26.1 60.1 %all-gather.6.cloned.1.call-done = bf16[1024,5120]{1,0:T(8,128)(2,1)} async-done(((bf16[256,5120]{1,0:T(8,128)(2,1)}), bf16[1024,5120]{1,0:T(8,128)(2,1)}) %all-gather.6.cloned.1.call-update) | async-done | bytes 10485776 | tf_op jit(solution)/shard_map/all_gather | solution.py:107
  86.2 7.0 fusion.39.v_ref
  93.3 5.8 convolution_add_fusion.5.k_ref
  99.1 16.4 %convolution_add_fusion.1.q_ref = f32[1024,1280]{1,0:T(8,128)S(1)} fusion(bf16[1024,5120]{1,0:T(8,128)(2,1)} %all-gather.6.cloned.1.call-done, bf16[5120,1280]{1,0:T(8,128)(2,1)S(1)} %bitcast.80, f32[1280]{0:T(1024)S(1)} %convert_element_type.207), kind=kOutput, calls=%fused_computation.34 | convolution fusion | flops 13423083520 | bytes 28840960 | tf_op jit(solution)/shard_map/dot_general | solution.py:96
  115.6 24.7 %attention.2 = (bf16[1024,1280]{1,0:T(8,128)(2,1)S(1)}, bf16[1024,256]{1,0:T(8,128)(2,1)S(1)}) custom-call(f32[1024,128]{1,0:T(8,128)S(1)} %get-tuple-element.82.cos_ref, f32[1024,128]{1,0:T(8,128)S(1)} %copy-done.3, f32[1024,1280]{1,0:T(8,128)S(1)} %convolution_add_fusion.1.q_ref, f32[1024,256]{1,0:T(8,128)S(1)} %convolution_add_fusion.5.k_ref, ...), custom_call_target="tpu_custom_call" | custom-call | flops 21474836480 | bytes 10485760 | tf_op jit(solution)/shard_map/attention/pallas_call | solution.py:77
  141.6 21.1 %convolution_convert_fusion.4 = bf16[512,5120]{1,0:T(8,128)(2,1)} fusion(bf16[512,1280]{1,0:T(8,128)(2,1)S(1)} %bitcast.76, bf16[1280,5120]{1,0:T(8,128)(2,1)S(1)} %bitcast.84), kind=kOutput, calls=%fused_computation.15 | convolution fusion | flops 6713507840 | bytes 19660800 | tf_op jit(solution)/shard_map/dot_general | solution.py:96
  166.2 13.6 %convolution_convert_fusion.3 = bf16[512,5120]{1,0:T(8,128)(2,1)} fusion(bf16[512,1280]{1,0:T(8,128)(2,1)} %bitcast.75, bf16[1280,5120]{1,0:T(8,128)(2,1)} %param.23), kind=kOutput, calls=%fused_computation.14 | convolution fusion | flops 6713507840 | bytes 19660800 | tf_op jit(solution)/shard_map/dot_general | solution.py:96
  179.9 7.0 fusion.40.v_ref
  186.9 5.6 convolution_add_fusion.3.k_ref
  192.6 14.1 %convolution_add_fusion.q_ref = f32[1024,1280]{1,0:T(8,128)S(1)} fusion(bf16[1024,5120]{1,0:T(8,128)(2,1)S(1)} %copy-done.20, bf16[5120,1280]{1,0:T(8,128)(2,1)S(1)} %bitcast.82, f32[1280]{0:T(1024)S(1)} %convert_element_type.207), kind=kOutput, calls=%fused_computation.33 | convolution fusion | flops 13423083520 | bytes 28840960 | tf_op jit(solution)/shard_map/dot_general | solution.py:96
  206.7 24.8 %attention.3 = (bf16[1024,1280]{1,0:T(8,128)(2,1)S(1)}, bf16[1024,256]{1,0:T(8,128)(2,1)S(1)}) custom-call(f32[1024,128]{1,0:T(8,128)S(1)} %get-tuple-element.84.cos_ref, f32[1024,128]{1,0:T(8,128)S(1)} %copy-done.2, f32[1024,1280]{1,0:T(8,128)S(1)} %convolution_add_fusion.q_ref, f32[1024,256]{1,0:T(8,128)S(1)} %convolution_add_fusion.3.k_ref, ...), custom_call_target="tpu_custom_call" | custom-call | flops 21474836480 | bytes 10485760 | tf_op jit(solution)/shard_map/attention/pallas_call | solution.py:77
  238.6 20.0 %reduce-scatter.12.cloned.1.call-done = bf16[128,5120]{1,0:T(8,128)(2,1)} async-done(((bf16[512,5120]{1,0:T(8,128)(2,1)}), bf16[128,5120]{1,0:T(8,128)(2,1)}) %reduce-scatter.12.cloned.1.call-update) | async-done | bytes 1310736 | tf_op jit(solution)/shard_map/reduce_scatter | solution.py:110
  264.3 19.8 %convolution_convert_fusion = bf16[1024,5120]{1,0:T(8,128)(2,1)} fusion(bf16[1024,1280]{1,0:T(8,128)(2,1)} %copy-done.10, bf16[1280,5120]{1,0:T(8,128)(2,1)} %param.23), kind=kOutput, calls=%fused_computation.11 | convolution fusion | flops 13427015680 | bytes 26214400 | tf_op jit(solution)/shard_map/dot_general | solution.py:96
  284.3 14.8 %all-gather.10.cloned.1.call-done = bf16[512,5120]{1,0:T(8,128)(2,1)} async-done(((bf16[128,5120]{1,0:T(8,128)(2,1)}), bf16[512,5120]{1,0:T(8,128)(2,1)}) %all-gather.10.cloned.1.call-update) | async-done | bytes 5242896 | tf_op jit(solution)/shard_map/all_gather | solution.py:107
  299.1 45.9 %fusion.44 = f32[512,6912]{1,0:T(8,128)} fusion(bf16[512,5120]{1,0:T(8,128)(2,1)} %all-gather.10.cloned.1.call-done, bf16[5120,6912]{1,0:T(8,128)(2,1)} %param.25), kind=kOutput, calls=%fused_computation.91 | convolution fusion | flops 36238786560 | bytes 90177536 | tf_op jit(solution)/shard_map/dot_general | solution.py:96
  345.0 48.9 %multiply_convert_fusion.2 = bf16[512,6912]{1,0:T(8,128)(2,1)} fusion(f32[512,6912]{1,0:T(8,128)} %fusion.44, bf16[512,5120]{1,0:T(8,128)(2,1)} %all-gather.10.cloned.1.call-done, bf16[5120,6912]{1,0:T(8,128)(2,1)} %param.26), kind=kOutput, calls=%fused_computation.10 | convolution fusion | flops 36260020224 | bytes 97255424 | tf_op jit(solution)/shard_map/dot_general | solution.py:96
  393.9 46.2 %fusion.45 = f32[512,6912]{1,0:T(8,128)} fusion(bf16[512,5120]{1,0:T(8,128)(2,1)} %all-gather.12.cloned.1.call-done, bf16[5120,6912]{1,0:T(8,128)(2,1)} %param.25), kind=kOutput, calls=%fused_computation.92 | convolution fusion | flops 36238786560 | bytes 90177536 | tf_op jit(solution)/shard_map/dot_general | solution.py:96
  447.7 49.1 %multiply_convert_fusion.1 = bf16[512,6912]{1,0:T(8,128)(2,1)} fusion(f32[512,6912]{1,0:T(8,128)} %fusion.45, bf16[512,5120]{1,0:T(8,128)(2,1)} %all-gather.12.cloned.1.call-done, bf16[5120,6912]{1,0:T(8,128)(2,1)} %param.26), kind=kOutput, calls=%fused_computation.9 | convolution fusion | flops 36260020224 | bytes 97255424 | tf_op jit(solution)/shard_map/dot_general | solution.py:96
  496.8 45.4 %convolution_convert_fusion.2 = bf16[512,5120]{1,0:T(8,128)(2,1)} fusion(bf16[512,6912]{1,0:T(8,128)(2,1)} %multiply_convert_fusion.2, bf16[6912,5120]{1,0:T(8,128)(2,1)} %param.27), kind=kOutput, calls=%fused_computation.13 | convolution fusion | flops 36241408000 | bytes 83099648 | tf_op jit(solution)/shard_map/dot_general | solution.py:96
  542.2 45.8 %convolution_convert_fusion.1 = bf16[512,5120]{1,0:T(8,128)(2,1)} fusion(bf16[512,6912]{1,0:T(8,128)(2,1)} %multiply_convert_fusion.1, bf16[6912,5120]{1,0:T(8,128)(2,1)} %param.27), kind=kOutput, calls=%fused_computation.12 | convolution fusion | flops 36241408000 | bytes 83099648 | tf_op jit(solution)/shard_map/dot_general | solution.py:96
  588.1 82.4 %fusion.46 = f32[1024,6912]{1,0:T(8,128)} fusion(bf16[1024,5120]{1,0:T(8,128)(2,1)} %all-gather.14.cloned.1.call-done, bf16[5120,6912]{1,0:T(8,128)(2,1)} %param.25), kind=kOutput, calls=%fused_computation.93 | convolution fusion | flops 72477573120 | bytes 109576192 | tf_op jit(solution)/shard_map/dot_general | solution.py:96
  670.6 85.2 %multiply_convert_fusion = bf16[1024,6912]{1,0:T(8,128)(2,1)} fusion(f32[1024,6912]{1,0:T(8,128)} %fusion.46, bf16[1024,5120]{1,0:T(8,128)(2,1)} %all-gather.14.cloned.1.call-done, bf16[5120,6912]{1,0:T(8,128)(2,1)} %param.26), kind=kOutput, calls=%fused_computation | convolution fusion | flops 72520040448 | bytes 123731968 | tf_op jit(solution)/shard_map/dot_general | solution.py:96
  755.7 24.7 %fusion.17 = bf16[1024,1280]{1,0:T(8,128)(2,1)} fusion(bf16[1024,6912]{1,0:T(8,128)(2,1)} %multiply_convert_fusion, bf16[6912,5120]{1,0:T(8,128)(2,1)} %param.27), kind=kOutput, calls=%fused_computation.41 | convolution fusion | flops 18120704000 | bytes 34471936 | tf_op jit(solution)/shard_map/dot_general | solution.py:96
  780.5 25.1 %fusion.20 = bf16[1024,1280]{1,0:T(8,128)(2,1)} fusion(bf16[1024,6912]{1,0:T(8,128)(2,1)} %multiply_convert_fusion, bf16[6912,5120]{1,0:T(8,128)(2,1)} %param.27), kind=kOutput, calls=%fused_computation.42 | convolution fusion | flops 18120704000 | bytes 34471936 | tf_op jit(solution)/shard_map/dot_general | solution.py:96
  805.7 5.5 reduce-scatter.20.cloned.1.call-done
  811.2 24.7 %fusion.23 = bf16[1024,1280]{1,0:T(8,128)(2,1)} fusion(bf16[1024,6912]{1,0:T(8,128)(2,1)} %multiply_convert_fusion, bf16[6912,5120]{1,0:T(8,128)(2,1)} %param.27), kind=kOutput, calls=%fused_computation.43 | convolution fusion | flops 18120704000 | bytes 34471936 | tf_op jit(solution)/shard_map/dot_general | solution.py:96
  836.0 8.1 reduce-scatter.22.cloned.1.call-done
  844.2 25.0 %fusion.26 = bf16[1024,1280]{1,0:T(8,128)(2,1)} fusion(bf16[1024,6912]{1,0:T(8,128)(2,1)} %multiply_convert_fusion, bf16[6912,5120]{1,0:T(8,128)(2,1)} %param.27), kind=kOutput, calls=%fused_computation.44 | convolution fusion | flops 18120704000 | bytes 34471936 | tf_op jit(solution)/shard_map/dot_general | solution.py:96
  869.1 8.0 reduce-scatter.24.cloned.1.call-done
  882.7 4.6 fusion.32
  888.9 21.7 %reduce-scatter.26.cloned.1.call-done = bf16[256,1280]{1,0:T(8,128)(2,1)} async-done(((bf16[1024,1280]{1,0:T(8,128)(2,1)}), bf16[256,1280]{1,0:T(8,128)(2,1)}) %reduce-scatter.26.cloned.1.call-update) | async-done | bytes 655376 | tf_op jit(solution)/shard_map/reduce_scatter | solution.py:110
  (146 shorter events, 51.8 us)
Async XLA Ops:
  7.2 79.0 %copy-start = (bf16[5120,256]{1,0:T(8,128)(2,1)S(1)}, bf16[5120,256]{1,0:T(8,128)(2,1)}, u32[]{:S(2)}) copy-start(bf16[5120,256]{1,0:T(8,128)(2,1)} %param.21) | copy-start | bytes 7864324
  7.2 79.0 %all-gather.6.cloned.1.call-start = ((), (), s32[]{:S(2)}) async-start(), calls=%async_computation.9 | async-start | bytes 13107200 | tf_op jit(solution)/shard_map/all_gather | solution.py:107
  14.5 165.3 %all-gather.8.cloned.1.call-start = ((), (), s32[]{:S(2)}) async-start(), calls=%async_computation.11 | async-start | bytes 13107200 | tf_op jit(solution)/shard_map/all_gather | solution.py:107
  19.4 213.7 %reduce-scatter.10.cloned.1.call-start = ((), (), s32[]{:S(2)}) async-start(), calls=%async_computation.10 | async-start | bytes 6553600 | tf_op jit(solution)/shard_map/reduce_scatter | solution.py:110
  86.2 12.9 %slice-start = ((s8[13107200]{0:T(1024)(128)(4,1)}), s8[4194304]{0:T(1024)(128)(4,1)S(1)}, s32[]{:S(2)}) async-start(s8[13107200]{0:T(1024)(128)(4,1)} %bitcast.79), calls=%async_computation.23 | async-start | bytes 8388608
  86.2 12.9 %slice-start.1 = ((s8[13107200]{0:T(1024)(128)(4,1)}), s8[4194304]{0:T(1024)(128)(4,1)S(1)}, s32[]{:S(2)}) async-start(s8[13107200]{0:T(1024)(128)(4,1)} %bitcast.79), calls=%async_computation.24 | async-start | bytes 8388608
  93.2 22.3 %copy-start.4 = (bf16[1024,256]{1,0:T(8,128)(2,1)}, bf16[1024,256]{1,0:T(8,128)(2,1)S(1)}, u32[]{:S(2)}) copy-start(bf16[1024,256]{1,0:T(8,128)(2,1)S(1)} %fusion.39.v_ref) | copy-start | bytes 1572868
  99.1 16.4 %copy-start.3 = (f32[1024,128]{1,0:T(8,128)S(1)}, f32[1024,128]{1,0:T(8,128)}, u32[]{:S(2)}) copy-start(f32[1024,128]{1,0:T(8,128)} %get-tuple-element.83.sin_ref) | copy-start | bytes 1572868
  115.5 26.1 %slice-start.8 = ((s8[13107200]{0:T(1024)(128)(4,1)}), s8[4194304]{0:T(1024)(128)(4,1)S(1)}, s32[]{:S(2)}) async-start(s8[13107200]{0:T(1024)(128)(4,1)} %bitcast.83), calls=%async_computation.31 | async-start | bytes 8388608
  115.6 26.1 %slice-start.9 = ((s8[13107200]{0:T(1024)(128)(4,1)}), s8[4194304]{0:T(1024)(128)(4,1)S(1)}, s32[]{:S(2)}) async-start(s8[13107200]{0:T(1024)(128)(4,1)} %bitcast.83), calls=%async_computation.32 | async-start | bytes 8388608
  115.6 26.0 %slice-start.10 = ((s8[13107200]{0:T(1024)(128)(4,1)}), s8[4194304]{0:T(1024)(128)(4,1)S(1)}, s32[]{:S(2)}) async-start(s8[13107200]{0:T(1024)(128)(4,1)} %bitcast.83), calls=%async_computation.33 | async-start | bytes 8388608
  115.6 26.0 %slice-start.11 = ((s8[13107200]{0:T(1024)(128)(4,1)}), s8[524288]{0:T(1024)(128)(4,1)S(1)}, s32[]{:S(2)}) async-start(s8[13107200]{0:T(1024)(128)(4,1)} %bitcast.83), calls=%async_computation.34 | async-start | bytes 1048576
  162.8 95.9 %reduce-scatter.12.cloned.1.call-start = ((), (), s32[]{:S(2)}) async-start(), calls=%async_computation.13 | async-start | bytes 6553600 | tf_op jit(solution)/shard_map/reduce_scatter | solution.py:110
  163.5 97.4 %copy-start.15 = (f32[5120]{0:T(1024)}, f32[5120]{0:T(1024)S(1)}, u32[]{:S(2)}) copy-start(f32[5120]{0:T(1024)S(1)} %convert_element_type.221) | copy-start | bytes 61444
  179.8 119.3 %all-gather.10.cloned.1.call-start = ((), (), s32[]{:S(2)}) async-start(), calls=%async_computation.12 | async-start | bytes 6553600 | tf_op jit(solution)/shard_map/all_gather | solution.py:107
  179.9 12.7 %slice-start.4 = ((s8[13107200]{0:T(1024)(128)(4,1)}), s8[4194304]{0:T(1024)(128)(4,1)S(1)}, s32[]{:S(2)}) async-start(s8[13107200]{0:T(1024)(128)(4,1)} %bitcast.81), calls=%async_computation.27 | async-start | bytes 8388608
  186.9 19.8 %copy-start.8 = (bf16[1024,256]{1,0:T(8,128)(2,1)}, bf16[1024,256]{1,0:T(8,128)(2,1)S(1)}, u32[]{:S(2)}) copy-start(bf16[1024,256]{1,0:T(8,128)(2,1)S(1)} %fusion.40.v_ref) | copy-start | bytes 1572868
  192.6 14.1 %copy-start.2 = (f32[1024,128]{1,0:T(8,128)S(1)}, f32[1024,128]{1,0:T(8,128)}, u32[]{:S(2)}) copy-start(f32[1024,128]{1,0:T(8,128)} %get-tuple-element.85.sin_ref) | copy-start | bytes 1572868
  238.6 155.4 %all-gather.12.cloned.1.call-start = ((), (), s32[]{:S(2)}) async-start(), calls=%async_computation.14 | async-start | bytes 6553600 | tf_op jit(solution)/shard_map/all_gather | solution.py:107
  264.2 175.9 %reduce-scatter.14.cloned.1.call-start = ((), (), s32[]{:S(2)}) async-start(), calls=%async_computation.15 | async-start | bytes 13107200 | tf_op jit(solution)/shard_map/reduce_scatter | solution.py:110
  284.1 303.9 %all-gather.14.cloned.1.call-start = ((), (), s32[]{:S(2)}) async-start(), calls=%async_computation.16 | async-start | bytes 13107200 | tf_op jit(solution)/shard_map/all_gather | solution.py:107
  447.7 222.8 %reduce-scatter.16.cloned.1.call-start = ((), (), s32[]{:S(2)}) async-start(), calls=%async_computation.17 | async-start | bytes 6553600 | tf_op jit(solution)/shard_map/reduce_scatter | solution.py:110
  588.0 192.4 %reduce-scatter.18.cloned.1.call-start = ((), (), s32[]{:S(2)}) async-start(), calls=%async_computation.18 | async-start | bytes 6553600 | tf_op jit(solution)/shard_map/reduce_scatter | solution.py:110
  670.5 140.6 %reduce-scatter.20.cloned.1.call-start = ((), (), s32[]{:S(2)}) async-start(), calls=%async_computation.19 | async-start | bytes 3276800 | tf_op jit(solution)/shard_map/reduce_scatter | solution.py:110
  780.5 63.6 %reduce-scatter.22.cloned.1.call-start = ((), (), s32[]{:S(2)}) async-start(), calls=%async_computation.20 | async-start | bytes 3276800 | tf_op jit(solution)/shard_map/reduce_scatter | solution.py:110
  811.2 66.0 %reduce-scatter.24.cloned.1.call-start = ((), (), s32[]{:S(2)}) async-start(), calls=%async_computation.21 | async-start | bytes 3276800 | tf_op jit(solution)/shard_map/reduce_scatter | solution.py:110
  844.1 33.1 %copy-start.5 = (bf16[1024,256]{1,0:T(8,128)(2,1)S(1)}, bf16[1024,256]{1,0:T(8,128)(2,1)}, u32[]{:S(2)}) copy-start(bf16[1024,256]{1,0:T(8,128)(2,1)} %copy-done.4) | copy-start | bytes 1572868
  844.1 33.2 %copy-start.9 = (bf16[1024,256]{1,0:T(8,128)(2,1)S(1)}, bf16[1024,256]{1,0:T(8,128)(2,1)}, u32[]{:S(2)}) copy-start(bf16[1024,256]{1,0:T(8,128)(2,1)} %copy-done.8) | copy-start | bytes 1572868
  844.1 33.3 %copy-start.7 = (bf16[1024,256]{1,0:T(8,128)(2,1)S(1)}, bf16[1024,256]{1,0:T(8,128)(2,1)}, u32[]{:S(2)}) copy-start(bf16[1024,256]{1,0:T(8,128)(2,1)} %copy-done.6) | copy-start | bytes 1572868
  844.1 66.5 %reduce-scatter.26.cloned.1.call-start = ((), (), s32[]{:S(2)}) async-start(), calls=%async_computation.22 | async-start | bytes 3276800 | tf_op jit(solution)/shard_map/reduce_scatter | solution.py:110
  887.3 23.4 %copy-start.12 = (bf16[256,5120]{1,0:T(8,128)(2,1)S(1)}, bf16[256,5120]{1,0:T(8,128)(2,1)}, u32[]{:S(2)}) copy-start(bf16[256,5120]{1,0:T(8,128)(2,1)} %copy-done.11) | copy-start | bytes 7864324
  887.3 23.4 %copy-start.14 = (bf16[256,1280]{1,0:T(8,128)(2,1)S(1)}, bf16[256,1280]{1,0:T(8,128)(2,1)}, u32[]{:S(2)}) copy-start(bf16[256,1280]{1,0:T(8,128)(2,1)} %reduce-scatter.20.cloned.1.call-done) | copy-start | bytes 1966084
  (18 other events, 79.4 us)
Sparse Core Ops, SparseCore 0:
  14.6 71.5 all-gather.5
  87.7 68.7 all-gather.7
  162.9 46.6 reduce-scatter.9
  212.0 46.6 reduce-scatter.11
  260.6 38.4 all-gather.9
  300.5 38.4 all-gather.11
  341.6 79.6 reduce-scatter.13
  447.8 68.7 all-gather.13
  588.2 46.5 reduce-scatter.15
  670.6 46.6 reduce-scatter.17
  780.6 30.5 reduce-scatter.19
  813.5 30.5 reduce-scatter.21
  846.6 30.5 reduce-scatter.23
  880.1 30.5 reduce-scatter.25
